TPU v7x, 32 devices: a whole 2x2x4 slice. The times are simulated.
32 devices in a mesh: groups: 2 (over y), tp: 4 (over z), tq: 2 (over x), tr: 2 (over core).
Axes of the slice: x: 2, y: 2, z: 4, core: 2. Of those that a mesh axis runs over, the one named last changes fastest.
Arguments:
- attn_heads: bfloat16 [128, 16384], P('groups', ('tp', 'tq', 'tr')), parts along dimension 0, may hold values from -6 to 6
- residual: bfloat16 [128, 16384], P('groups', ('tp', 'tq', 'tr')), parts along dimension 0, may hold values from -120 to 120
- o_weight: bfloat16 [16384, 16384], P(('tp', 'tq', 'tr')), may hold values from -0.0625 to 0.0625
- norm_gain: bfloat16 [16384], P(('tp', 'tq', 'tr')), may hold values from 0.099609375 to 1.8984375
- q_weight: bfloat16 [16384, 16384], P(None, ('tp', 'tq', 'tr')), may hold values from -0.046875 to 0.046875
Outputs:
- hidden: bfloat16 [128, 16384], P('groups', ('tp', 'tq', 'tr')), parts along dimension 0
- peak_value: float32 [128], P('groups'), parts along dimension 0
- query: bfloat16 [128, 16384], P('groups', ('tp', 'tq', 'tr')), parts along dimension 0
There are 2 independent parts, one for each index of `groups`. A program takes and returns all parts, laid end to end along the dimension named above; an argument that names none is the same for every part. Nothing has to cross between parts.
All inputs are finite; a program needn't handle non-finite values. Where the computation divides by a largest or mean magnitude, that divisor is 1e-20 or more.
Results may differ from a plain program's by a relative error of at most 0.0095.
Values may be sent and summed in bfloat16 or wider, within the bound.
A program may use at most 128 MiB of HBM per device.

v0:
```python
import jax
import jax.numpy as jnp
from jax import lax
from jax.sharding import PartitionSpec as P

D = 16384


def merged(array, axis, combine):
    everything = jax.tree.map(lambda part: lax.all_gather(part, axis), array)
    leading = jax.tree.map(lambda part: part[0], everything)

    def step(k, so_far):
        return combine(so_far, jax.tree.map(lambda part: part[k], everything))

    return lax.fori_loop(1, lax.axis_size(axis), step, leading)


def combine_stats(lhs_stats, rhs_stats):
    return (lhs_stats[0] + rhs_stats[0], jnp.maximum(lhs_stats[1], rhs_stats[1]))


def body(attn_heads, residual, o_weight, norm_gain, q_weight):
    terms = jnp.dot(attn_heads, o_weight, preferred_element_type=jnp.float32)
    attn_total = lax.psum_scatter(terms, ("tp", "tq", "tr"), scatter_dimension=1, tiled=True)
    hidden = (residual.astype(jnp.float32) + attn_total).astype(jnp.bfloat16)
    widened = hidden.astype(jnp.float32)
    gained = widened * norm_gain.astype(jnp.float32)
    squares = jnp.sum(widened * widened, axis=1)
    local_top = jnp.max(jnp.abs(gained), axis=1)
    row_total, global_top = merged((squares, local_top), ("tp", "tq", "tr"), combine_stats)
    inv_rms = lax.rsqrt(row_total / D + 1e-05)
    normed = gained * inv_rms[:, None]
    peak_value = global_top * inv_rms
    quantized = (normed * (448.0 / (peak_value + 1e-06))[:, None]).astype(jnp.bfloat16)
    projected = jnp.dot(
        lax.all_gather(quantized, ("tp", "tq", "tr"), axis=1, tiled=True),
        q_weight,
        preferred_element_type=jnp.float32,
    )
    query = (projected * ((peak_value + 1e-06) / 448.0)[:, None]).astype(jnp.bfloat16)
    return (hidden, peak_value, query)


def solution(mesh):
    placed = (
        P("groups", ("tp", "tq", "tr")),
        P("groups", ("tp", "tq", "tr")),
        P(("tp", "tq", "tr"), None),
        P(("tp", "tq", "tr")),
        P(None, ("tp", "tq", "tr")),
    )
    return jax.shard_map(
        body,
        mesh=mesh,
        in_specs=placed,
        out_specs=(P("groups", ("tp", "tq", "tr")), P("groups"), P("groups", ("tp", "tq", "tr"))),
        check_vma=False,
    )
```

profile of v0, /device:TPU:0, one launch (start us, length us, event | category | flops | bytes accessed | tf_op | source)
XLA Modules:
  0.0 195.9 jit_solution(17033480486066413661)
XLA Ops:
  7.2 0.0 copy-start
  7.2 0.0 copy-start.5
  7.2 0.0 copy-start.3
  7.2 0.0 copy-start.2
  7.2 0.0 reduce-scatter.2.cloned.1.call-start
  7.3 0.8 copy-done
  8.1 15.5 %fusion.9 = f32[64,16384]{1,0:T(8,128)} fusion(bf16[64,1024]{1,0:T(8,128)(2,1)S(1)} %copy-done, bf16[1024,16384]{1,0:T(8,128)(2,1)} %param.9), kind=kOutput, calls=%fused_computation.17 | convolution fusion | flops 2147483648 | bytes 37879808 | tf_op jit(solution)/shard_map/dot_general | solution.py:24
  23.6 0.0 reduce-scatter.2.cloned.1.call-update
  23.6 0.0 all-gather.4.cloned.1.call-start
  23.7 0.0 copy-done.3
  23.7 0.0 copy-done.5
  23.7 0.6 dynamic-slice
  25.0 74.3 %reduce-scatter.2.cloned.1.call-done = f32[64,1024]{1,0:T(8,128)} async-done(((f32[64,16384]{1,0:T(8,128)}), f32[64,1024]{1,0:T(8,128)}) %reduce-scatter.2.cloned.1.call-update) | async-done | bytes 262160 | tf_op jit(solution)/shard_map/reduce_scatter | solution.py:25
  99.3 0.0 copy-done.2
  99.3 1.1 fusion.3
  100.4 0.0 copy-start.1
  100.4 0.2 dynamic-update-slice
  100.7 0.2 dynamic-update-slice.1
  100.9 30.0 %all-reduce.2 = (f32[1024]{0:T(1024)S(1)}, f32[1024]{0:T(1024)S(1)}) all-reduce(f32[1024]{0:T(1024)S(1)} %dynamic-update-slice, f32[1024]{0:T(1024)S(1)} %dynamic-update-slice.1), channel_id=2, replica_groups=mesh['groups'=2,'tp'=4,'tq'=2,'tr'=2] {'tp','tq','tr'}, use_global_device_ids=true, to_apply=%add | all-reduce | flops 2048 | bytes 16384
  130.9 0.1 reshape.10
  131.0 0.1 reshape.11
  131.0 0.6 while.17
  131.6 0.0 copy-start.4
  131.7 0.8 fusion.5
  132.4 0.0 all-gather.4.cloned.1.call-update
  132.4 38.9 %all-gather.4.cloned.1.call-done = bf16[64,16384]{1,0:T(8,128)(2,1)} async-done(((bf16[64,1024]{1,0:T(8,128)(2,1)}), bf16[64,16384]{1,0:T(8,128)(2,1)}) %all-gather.4.cloned.1.call-update) | async-done | bytes 2097168 | tf_op jit(solution)/shard_map/all_gather | solution.py:37
  171.3 17.8 %fusion = bf16[64,1024]{1,0:T(8,128)(2,1)} fusion(bf16[64,16384]{1,0:T(8,128)(2,1)} %all-gather.4.cloned.1.call-done, bf16[16384,1024]{1,0:T(8,128)(2,1)} %param.11, f32[64]{0:T(128)S(1)} %get-tuple-element.152), kind=kOutput, calls=%fused_computation.3 | convolution fusion | flops 2147614720 | bytes 35782912 | tf_op jit(solution)/shard_map/dot_general | solution.py:36
  189.1 0.0 copy-done.1
  189.1 0.0 copy-done.4
  (22 shorter events, 0.3 us)
Async XLA Ops:
  7.2 0.9 copy-start
  7.2 16.5 %copy-start.5 = (u32[32]{0:T(128)S(1)}, u32[32]{0:T(128)}, u32[]{:S(2)}) copy-start(u32[32]{0:T(128)} %constant.55) | copy-start | bytes 388
  7.2 16.5 %copy-start.3 = (bf16[1024]{0:T(1024)(128)(2,1)S(1)}, bf16[1024]{0:T(1024)(128)(2,1)}, u32[]{:S(2)}) copy-start(bf16[1024]{0:T(1024)(128)(2,1)} %param.10) | copy-start | bytes 6148
  7.2 92.1 %copy-start.2 = (bf16[64,1024]{1,0:T(8,128)(2,1)S(1)}, bf16[64,1024]{1,0:T(8,128)(2,1)}, u32[]{:S(2)}) copy-start(bf16[64,1024]{1,0:T(8,128)(2,1)} %param.8) | copy-start | bytes 393220
  7.2 92.1 %reduce-scatter.2.cloned.1.call-start = ((), (), s32[]{:S(2)}) async-start(), calls=%async_computation.1 | async-start | bytes 4456448 | tf_op jit(solution)/shard_map/reduce_scatter | solution.py:25
  23.6 147.7 %all-gather.4.cloned.1.call-start = ((), (), s32[]{:S(2)}) async-start(), calls=%async_computation.2 | async-start | bytes 2228224 | tf_op jit(solution)/shard_map/all_gather | solution.py:37
  100.4 88.7 %copy-start.1 = (bf16[64,1024]{1,0:T(8,128)(2,1)}, bf16[64,1024]{1,0:T(8,128)(2,1)S(1)}, u32[]{:S(2)}) copy-start(bf16[64,1024]{1,0:T(8,128)(2,1)S(1)} %get-tuple-element.154) | copy-start | bytes 393220
  131.6 57.4 %copy-start.4 = (f32[64]{0:T(128)}, f32[64]{0:T(128)S(1)}, u32[]{:S(2)}) copy-start(f32[64]{0:T(128)S(1)} %get-tuple-element.153) | copy-start | bytes 772
Sparse Core Ops, SparseCore 0:
  23.7 75.5 reduce-scatter.1
  132.6 38.6 all-gather.3
where the time goes:
time: 196 us
  waiting for transfers between devices  113 us (58%)
  matrix products  33.3 us (17%)
  blocking collectives  30 us (15%)
  between operations  14.8 us (8%)
  other arithmetic  2.15 us (1%)
  local copies, waits for them, and re-layouts  2.06 us (1%)
    reduce_scatter x1, waiting for transfers between devices, body(): lax.psum_scatter(terms, ('tp', 'tq', 'tr'), scatter_dimension=1, tiled=True)  74.3 us
    all_gather x1, waiting for transfers between devices, body(): lax.all_gather(quantized, ('tp', 'tq', 'tr'), axis=1, tiled=True)  38.9 us
    unnamed x1, blocking collectives  30 us
    dot_general x1, matrix products, body(): jnp.dot(lax.all_gather(quantized, ('tp', 'tq', 'tr'), axis=1, tiled=True)...  17.8 us
    dot_general x1, matrix products, body(): terms = jnp.dot(attn_heads, o_weight, preferred_element_type=jnp.float32)  15.5 us
  transfers between devices with their start and end apart: 2, of which 2 were waited for; matrix products, arithmetic and copies ran while one was open for 0% of the time, Pallas kernels for 0%

commit v1 on v0

v1 whole, which is shorter than its diff:
```python
import functools

import jax
import jax.numpy as jnp
from jax import lax
from jax.experimental import pallas as pl
from jax.experimental.pallas import tpu as pltpu
from jax.sharding import PartitionSpec as P

MESH = pl.DeviceIdType.MESH
F32, BF16 = jnp.float32, jnp.bfloat16
SLOTS = 8
LAG = 4


def flip(index, mask):
    bit = 1
    while bit <= mask:
        if mask & bit:
            index = index + bit - 2 * bit * ((index // bit) % 2)
        bit *= 2
    return index


def multiply(lhs_ref, rhs_ref, put):
    width = rhs_ref.shape[1]
    tile = min(width, 512)

    def step(j, carry):
        columns = pl.ds(pl.multiple_of(j * tile, tile), tile)
        put(columns, jnp.dot(lhs_ref[...], rhs_ref[:, columns], preferred_element_type=F32))
        return carry

    lax.fori_loop(0, width // tile, step, 0)


def kernel(
    Z, X, C, D,
    attn_hbm, res_hbm, o_hbm, gain_ref, q_hbm,
    hidden_hbm, peak_ref, query_ref,
    attn, res, hid, obuf, qbuf, gath, acc, total,
    core_out, core_in, x_out, x_in, z_out, z_in, stat_out, stat_in,
    small_sem, o_sem, q_sem, core_s, core_r, x_s, x_r, z_s, z_r, g_s, g_r, st_s, st_r,
):
    TOK, F = res.shape
    n = Z * X * C
    me = {"tp": lax.axis_index("tp"), "tq": lax.axis_index("tq"), "tr": lax.axis_index("tr")}

    def block_of(dz, dx, dc):
        return (flip(me["tp"], dz) * X + flip(me["tq"], dx)) * C + flip(me["tr"], dc)

    def send(src, dst, s, r, axis, d):
        copy = pltpu.make_async_remote_copy(
            src_ref=src, dst_ref=dst, send_sem=s, recv_sem=r,
            device_id={axis: flip(me[axis], d)}, device_id_type=MESH,
        )
        copy.start()
        sent.append(copy)
        return copy

    sent = []
    groups = [(dz, dx) for dz in reversed(range(Z)) for dx in reversed(range(X))]
    order = [(dz, dx, dc) for dz, dx in groups for dc in reversed(range(C))]

    def o_copy(b):
        start = pl.multiple_of(block_of(*order[b]) * F, F)
        return pltpu.make_async_copy(
            o_hbm.at[:, pl.ds(start, F)], obuf.at[b % SLOTS], o_sem.at[b % SLOTS])

    def slot(dz, dx, dc):
        return (dz * X + dx) * C + dc

    def blocks_from_z(dz):
        later = [(dz, dx, 0) for dx in range(1, X)]
        return later + [(dz, dx, dc) for dx in range(X) for dc in range(1, C)]

    use = [(0, 0, 0)]
    for dz in range(1, Z):
        use += [(dz, 0, 0)] + blocks_from_z(dz - 1)
    use += blocks_from_z(Z - 1)

    def q_copy(k):
        start = pl.multiple_of(block_of(*use[k]) * F, F)
        at = slot(*use[k])
        return pltpu.make_async_copy(q_hbm.at[pl.ds(start, F), :], qbuf.at[at], q_sem.at[at])

    attn_copy = pltpu.make_async_copy(attn_hbm, attn, small_sem.at[0])
    attn_copy.start()
    for b in range(min(SLOTS, n)):
        o_copy(b).start()
    res_copy = pltpu.make_async_copy(res_hbm, res, small_sem.at[1])
    res_copy.start()

    barrier = pltpu.get_barrier_semaphore()
    for axis, size in (("tp", Z), ("tq", X), ("tr", C)):
        for d in range(1, size):
            pl.semaphore_signal(
                barrier, inc=1, device_id={axis: flip(me[axis], d)}, device_id_type=MESH)
    attn_copy.wait()

    core_copies, x_copies, z_copies = {}, {}, {}
    q_next = 0

    def after_core(i):
        dz, dx = groups[i]
        value = acc[i]
        for dc in range(1, C):
            core_copies[i, dc].wait_recv()
            value = value + core_in[i * (C - 1) + dc - 1].astype(F32)
        if dx:
            at = dz * (X - 1) + dx - 1
            x_out[at] = value.astype(BF16)
            x_copies[dz, dx] = send(x_out.at[at], x_in.at[at], x_s.at[at], x_r.at[at], "tq", dx)
        else:
            acc[i] = value

    def after_x(dz):
        i = groups.index((dz, 0))
        value = acc[i]
        for dx in range(1, X):
            x_copies[dz, dx].wait_recv()
            value = value + x_in[dz * (X - 1) + dx - 1].astype(F32)
        if dz:
            z_out[dz - 1] = value.astype(BF16)
            z_copies[dz] = send(
                z_out.at[dz - 1], z_in.at[dz - 1], z_s.at[dz - 1], z_r.at[dz - 1], "tp", dz)
        else:
            total[...] = value

    pending = []
    for i, (dz, dx) in enumerate(groups):
        for dc in reversed(range(C)):
            b = i * C + C - 1 - dc
            o_copy(b).wait()
            rhs = obuf.at[b % SLOTS]
            if dc:
                at = i * (C - 1) + dc - 1

                def put(columns, product):
                    core_out[at, :, columns] = product.astype(BF16)

                multiply(attn, rhs, put)
                if b == 0:
                    pl.semaphore_wait(barrier, Z + X + C - 3)
                core_copies[i, dc] = send(
                    core_out.at[at], core_in.at[at], core_s.at[at], core_r.at[at], "tr", dc)
            else:

                def put(columns, product):
                    acc[i, :, columns] = product

                multiply(attn, rhs, put)
            if b + SLOTS < n:
                o_copy(b + SLOTS).start()
            else:
                q_copy(q_next).start()
                q_next += 1
        if i >= 1:
            after_core(i - 1)
            if groups[i - 1][1] == 0:
                pending.append((i - 1, groups[i - 1][0]))
        if pending and i - pending[0][0] >= LAG:
            after_x(pending.pop(0)[1])
    while q_next < n:
        q_copy(q_next).start()
        q_next += 1
    after_core(len(groups) - 1)
    pending.append((len(groups) - 1, 0))
    for _, dz in pending:
        after_x(dz)

    res_copy.wait()
    value = total[...]
    for dz in range(1, Z):
        z_copies[dz].wait_recv()
        value = value + z_in[dz - 1].astype(F32)
    hidden = (res[...].astype(F32) + value).astype(BF16)
    hid[...] = hidden
    widened = hidden.astype(F32)
    gained = widened * gain_ref[...].astype(F32)
    gath[0] = gained.astype(BF16)

    arrive = {}

    def forward(dz, dx):
        at = slot(dz, dx, 0)
        for dc in range(1, C):
            to = slot(dz, dx, dc)
            arrive[dz, dx, dc] = send(
                gath.at[at], gath.at[to], g_s.at[to], g_r.at[to], "tr", dc)

    def forward_x(dz):
        at = slot(dz, 0, 0)
        for dx in range(1, X):
            to = slot(dz, dx, 0)
            arrive[dz, dx, 0] = send(
                gath.at[at], gath.at[to], g_s.at[to], g_r.at[to], "tq", dx)

    for dz in range(1, Z):
        to = slot(dz, 0, 0)
        arrive[dz, 0, 0] = send(gath.at[0], gath.at[to], g_s.at[to], g_r.at[to], "tp", dz)
    forward_x(0)
    forward(0, 0)
    hidden_copy = pltpu.make_async_copy(hid, hidden_hbm, small_sem.at[2])
    hidden_copy.start()

    squares = jnp.sum(widened * widened, axis=1, keepdims=True)
    top = jnp.max(jnp.abs(gained), axis=1, keepdims=True)
    wide = jnp.concatenate(
        [jnp.broadcast_to(squares, (TOK, 128)), jnp.broadcast_to(top, (TOK, 128))], axis=0)
    stat = jnp.transpose(wide)[:8, :]
    lane = lax.broadcasted_iota(jnp.int32, stat.shape, 1)
    axes = (("tr", C), ("tq", X), ("tp", Z))
    first = {"tr": 0, "tq": C - 1, "tp": C + X - 2}
    stat_copies = {}

    def stat_send(stage, stat):
        axis, size = axes[stage]
        stat_out[stage] = stat
        for d in range(1, size):
            at = first[axis] + d - 1
            stat_copies[axis, d] = send(
                stat_out.at[stage], stat_in.at[at], st_s.at[at], st_r.at[at], axis, d)

    def stat_take(stage, stat):
        axis, size = axes[stage]
        for d in range(1, size):
            stat_copies[axis, d].wait_recv()
            other = stat_in[first[axis] + d - 1]
            stat = jnp.where(lane < TOK, stat + other, jnp.maximum(stat, other))
        return stat

    stat_send(0, stat)

    for k, at in enumerate(use):
        dz, dx, dc = at
        if k:
            arrive[at].wait_recv()
            if dc == 0:
                if dx == 0:
                    forward_x(dz)
                forward(dz, dx)
        q_copy(k).wait()
        if k == 0:

            def put(columns, product):
                total[:, columns] = product
        else:

            def put(columns, product):
                total[:, columns] += product

        multiply(gath.at[slot(*at)], qbuf.at[slot(*at)], put)
        if k in (1, 3):
            stage = 0 if k == 1 else 1
            stat = stat_take(stage, stat_out[stage])
            stat_send(stage + 1, stat)
    stat = stat_take(2, stat_out[2])
    scale = lax.rsqrt(stat / D + 1e-05)
    peak_ref[...] = pltpu.roll(stat, TOK, 1) * scale
    rows = jnp.transpose(jnp.broadcast_to(scale[:1, :], (128, 128)))[:TOK, :1]
    query_ref[...] = (total[...] * rows).astype(BF16)
    hidden_copy.wait()
    for copy in sent:
        copy.wait_send()


def body(sizes, attn_heads, residual, o_weight, norm_gain, q_weight):
    Z, X, C = sizes
    TOK, F = residual.shape
    K, D = o_weight.shape
    n = Z * X * C
    pairs = Z * X * (C - 1)
    dma = pltpu.SemaphoreType.DMA
    block = (TOK, F)
    hbm = pl.BlockSpec(memory_space=pl.ANY)
    vmem = pl.BlockSpec(memory_space=pltpu.VMEM)
    hops = C + X + Z - 3
    hidden, peak, query = pl.pallas_call(
        functools.partial(kernel, Z, X, C, D),
        name="decode",
        out_shape=(
            jax.ShapeDtypeStruct(block, BF16),
            jax.ShapeDtypeStruct((8, 128), F32),
            jax.ShapeDtypeStruct(block, BF16),
        ),
        in_specs=[hbm, hbm, hbm, vmem, hbm],
        out_specs=(hbm, vmem, vmem),
        scratch_shapes=[
            pltpu.VMEM((TOK, K), BF16),
            pltpu.VMEM(block, BF16),
            pltpu.VMEM(block, BF16),
            pltpu.VMEM((SLOTS, K, F), BF16),
            pltpu.VMEM((n, F, q_weight.shape[1]), BF16),
            pltpu.VMEM((n,) + block, BF16),
            pltpu.VMEM((Z * X,) + block, F32),
            pltpu.VMEM(block, F32),
            pltpu.VMEM((pairs,) + block, BF16),
            pltpu.VMEM((pairs,) + block, BF16),
            pltpu.VMEM((Z * (X - 1),) + block, BF16),
            pltpu.VMEM((Z * (X - 1),) + block, BF16),
            pltpu.VMEM((Z - 1,) + block, BF16),
            pltpu.VMEM((Z - 1,) + block, BF16),
            pltpu.VMEM((3, 8, 128), F32),
            pltpu.VMEM((hops, 8, 128), F32),
            dma((3,)), dma((SLOTS,)), dma((n,)),
            dma((pairs,)), dma((pairs,)),
            dma((Z * (X - 1),)), dma((Z * (X - 1),)),
            dma((Z - 1,)), dma((Z - 1,)),
            dma((n,)), dma((n,)),
            dma((hops,)), dma((hops,)),
        ],
        compiler_params=pltpu.CompilerParams(
            collective_id=0, has_side_effects=True, vmem_limit_bytes=66 * 1000 * 1000),
    )(attn_heads, residual, o_weight, norm_gain.reshape(1, F), q_weight)
    return hidden, peak[0, :TOK], query


def solution(mesh):
    split = ("tp", "tq", "tr")
    placed = (
        P("groups", split),
        P("groups", split),
        P(split, None),
        P(split),
        P(None, split),
    )
    return jax.shard_map(
        functools.partial(body, tuple(mesh.shape[axis] for axis in split)),
        mesh=mesh,
        in_specs=placed,
        out_specs=(P("groups", split), P("groups"), P("groups", split)),
        check_vma=False,
    )
```

time: 196 us -> 57.6 us (0.29)
  waiting for transfers between devices: 113 us -> 0 us
  Pallas kernels: 0 us -> 51.1 us
  matrix products: 33.3 us -> 0 us
  blocking collectives: 30 us -> 0 us
  between operations: 14.8 us -> 0.64 us
  local copies, waits for them, and re-layouts: 2.06 us -> 5.61 us
  other arithmetic: 2.15 us -> 0 us
    reduce_scatter x1 -> x0, waiting for transfers between devices: 74.3 us -> none  [body(): lax.psum_scatter(terms, ('tp', 'tq', 'tr'), scatter_dimension=1, tiled=True)]
    pallas_call x0 -> x1, Pallas kernels: none -> 51.1 us  [body(): pl.pallas_call(functools.partial(kernel, Z, X, C, D), name='decode', out_...]
    all_gather x1 -> x0, waiting for transfers between devices: 38.9 us -> none  [body(): lax.all_gather(quantized, ('tp', 'tq', 'tr'), axis=1, tiled=True)]
    dot_general x2 -> x0, matrix products: 33.3 us -> none  [the longest x1 17.8 us: body(): jnp.dot(lax.all_gather(quantized, ('tp', 'tq', 'tr'), axis=1, tiled=True)...]
    unnamed x1 -> x0, blocking collectives: 30 us -> none
  transfers between devices with their start and end apart: 2 -> 0, of which waited for: 2 -> 0; matrix products, arithmetic and copies ran while one was open for 0% -> 0% of each run, Pallas kernels for 0% -> 0%
where the time goes in v1:
time: 57.6 us; the launch traced here: 57.4 us
  Pallas kernels  51.1 us (89%)
  local copies, waits for them, and re-layouts  5.61 us (10%)
  between operations  0.64 us (1%)
    pallas_call x1, Pallas kernels, body(): pl.pallas_call(functools.partial(kernel, Z, X, C, D), name='decode', out_...  51.1 us
    unnamed x2, local copies, waits for them, and re-layouts  3.13 us
    reshape x1, local copies, waits for them, and re-layouts, body(): norm_gain.reshape(1, F)  1.28 us
    squeeze x1, local copies, waits for them, and re-layouts, body(): return (hidden, peak[0, :TOK], query)  1.2 us

profile of v1, /device:TPU:0, one launch (start us, length us, event | category | flops | bytes accessed | tf_op | source)
XLA Modules:
  0.0 57.4 jit_solution(11242646588891557465)
XLA Ops:
  0.6 1.3 %reshape.9.gain_ref = bf16[1,1024]{1,0:T(2,128)(2,1)} reshape(bf16[1024]{0:T(1024)(128)(2,1)} %param.8) | data formatting | bytes 4096 | tf_op jit(solution)/shard_map/reshape | solution.py:315
  1.9 51.1 %decode.1 = (bf16[64,1024]{1,0:T(8,128)(2,1)}, f32[8,128]{1,0:T(8,128)}, bf16[64,1024]{1,0:T(8,128)(2,1)}) custom-call(bf16[64,1024]{1,0:T(8,128)(2,1)} %attn_hbm.1, bf16[64,1024]{1,0:T(8,128)(2,1)} %res_hbm.1, bf16[1024,16384]{1,0:T(8,128)(2,1)} %o_hbm.1, bf16[1,1024]{1,0:T(2,128)(2,1)} %reshape.9.gain_ref, bf16[16384,1024]{1,0:T(8,128)(2,1)} %q_hbm.1), custom_call_target="tpu_custom_call" | custom-call | tf_op jit(solution)/shard_map/decode/pallas_call | solution.py:279
  53.1 1.2 %slice_bitcast_fusion = f32[64]{0:T(128)} fusion(f32[8,128]{1,0:T(8,128)} %get-tuple-element.7), kind=kLoop, calls=%fused_computation | loop fusion | bytes 512 | tf_op jit(solution)/shard_map/squeeze | solution.py:316
  54.3 1.6 %copy.10 = bf16[64,1024]{1,0:T(8,128)(2,1)} copy(bf16[64,1024]{1,0:T(8,128)(2,1)} %get-tuple-element.12) | data formatting | bytes 262144
  55.8 1.6 %copy.11 = bf16[64,1024]{1,0:T(8,128)(2,1)} copy(bf16[64,1024]{1,0:T(8,128)(2,1)} %get-tuple-element.14) | data formatting | bytes 262144

commit v2 on v1

v2 whole, which is shorter than its diff:
```python
import functools

import jax
import jax.numpy as jnp
from jax import lax
from jax.experimental import pallas as pl
from jax.experimental.pallas import tpu as pltpu
from jax.sharding import PartitionSpec as P

MESH = pl.DeviceIdType.MESH
F32, BF16 = jnp.float32, jnp.bfloat16
SLOTS = 8
PARTS = 2


def flip(index, mask):
    bit = 1
    while bit <= mask:
        if mask & bit:
            index = index + bit - 2 * bit * ((index // bit) % 2)
        bit *= 2
    return index


def multiply(lhs_ref, rhs_ref, put):
    width = rhs_ref.shape[1]
    tile = min(width, 512)

    def step(j, carry):
        columns = pl.ds(pl.multiple_of(j * tile, tile), tile)
        put(columns, jnp.dot(lhs_ref[...], rhs_ref[:, columns], preferred_element_type=F32))
        return carry

    lax.fori_loop(0, width // tile, step, 0)


def kernel(
    Z, X, C, D,
    attn_hbm, res_hbm, o_hbm, gain_ref, q_hbm,
    hidden_hbm, peak_ref, query_ref,
    attn, res, hid, obuf, qbuf, gath, acc, total,
    core_out, core_in, x_out, x_in, z_out, z_in, stat_out, stat_in,
    small_sem, o_sem, q_sem, core_s, core_r, x_s, x_r, z_s, z_r, g_s, g_r, f_s, st_s, st_r,
):
    TOK, F = res.shape
    n = Z * X * C
    me = {"tp": lax.axis_index("tp"), "tq": lax.axis_index("tq"), "tr": lax.axis_index("tr")}

    z = me["tp"]
    line = Z == 4
    inner = jnp.logical_or(z == 1, z == 2)
    outer = jnp.logical_or(z == 0, z == 3)
    rows = [pl.ds(h * (TOK // PARTS), TOK // PARTS) for h in range(PARTS)]
    halves = range(PARTS)

    def z_of(role):
        if line and role == 2:
            return 2 - z // 2
        if line and role == 3:
            return 3 - 3 * (z // 2)
        return flip(z, role)

    def block_of(role, dx, dc):
        return (z_of(role) * X + flip(me["tq"], dx)) * C + flip(me["tr"], dc)

    def remote(src, dst, s, r, axis, d):
        return pltpu.make_async_remote_copy(
            src_ref=src, dst_ref=dst, send_sem=s, recv_sem=r,
            device_id={axis: flip(me[axis], d)}, device_id_type=MESH,
        )

    def send(src, dst, s, r, axis, d, only=None):
        copy = remote(src, dst, s, r, axis, d)
        if only is None:
            copy.start()
        else:
            pl.when(only)(copy.start)
        sent.append((copy, only))
        return copy

    sent = []
    roles = list(reversed(range(Z)))
    groups = [(role, dx) for role in roles for dx in reversed(range(X))]
    order = [(role, dx, dc) for role, dx in groups for dc in reversed(range(C))]

    def o_copy(b):
        start = pl.multiple_of(block_of(*order[b]) * F, F)
        return pltpu.make_async_copy(
            o_hbm.at[:, pl.ds(start, F)], obuf.at[b % SLOTS], o_sem.at[b % SLOTS])

    def slot(role, dx, dc):
        return (role * X + dx) * C + dc

    plan = [("mul", (0, 0, 0))] + [("take", (0, 0, dc)) for dc in range(1, C)]
    plan += [("mul", (0, 0, dc)) for dc in range(1, C)]
    ready = []
    for role in range(1, Z + 1):
        new = [(role, 0, 0)] if role < Z else []
        new += [(role - 1, dx, 0) for dx in range(1, X)]
        for at in new:
            plan.append(("take", at))
            if ready:
                plan.append(("mul", ready.pop(0)))
        ready += new
        while len(ready) > len(new):
            plan.append(("mul", ready.pop(0)))
        later = [(role, 0, dc) for dc in range(1, C)] if role < Z else []
        later += [(role - 1, dx, dc) for dx in range(1, X) for dc in range(1, C)]
        ready += later
    taken = {at for what, at in plan if what == "take"}
    full = []
    for what, at in plan:
        if what == "mul" and at not in taken and at != (0, 0, 0):
            full.append(("take", at))
        full.append((what, at))
    for at in ready:
        if at not in taken:
            full.append(("take", at))
        full.append(("mul", at))
    plan = full
    use = [at for what, at in plan if what == "mul"]

    def q_copy(k):
        start = pl.multiple_of(block_of(*use[k]) * F, F)
        at = slot(*use[k])
        return pltpu.make_async_copy(q_hbm.at[pl.ds(start, F), :], qbuf.at[at], q_sem.at[at])

    attn_copy = pltpu.make_async_copy(attn_hbm, attn, small_sem.at[0])
    attn_copy.start()
    for b in range(min(SLOTS, n)):
        o_copy(b).start()
    res_copy = pltpu.make_async_copy(res_hbm, res, small_sem.at[1])
    res_copy.start()

    barrier = pltpu.get_barrier_semaphore()
    for axis, size in (("tp", Z), ("tq", X), ("tr", C)):
        for d in range(1, size):
            pl.semaphore_signal(
                barrier, inc=1, device_id={axis: flip(me[axis], d)}, device_id_type=MESH)
    attn_copy.wait()
    gain = gain_ref[...].reshape(1, F).astype(F32)

    core_copies, x_copies, z_copies = {}, {}, {}
    q_next = 0

    def after_core(i):
        role, dx = groups[i]
        for h in halves:
            value = acc[i, rows[h]]
            for dc in range(1, C):
                core_copies[i, dc, h].wait_recv()
                value = value + core_in[i * (C - 1) + dc - 1, rows[h]].astype(F32)
            if dx:
                at = role * (X - 1) + dx - 1
                x_out[at, rows[h]] = value.astype(BF16)
                x_copies[role, dx, h] = send(
                    x_out.at[at, rows[h]], x_in.at[at, rows[h]],
                    x_s.at[at, h], x_r.at[at, h], "tq", dx)
            else:
                acc[i, rows[h]] = value

    def z_send(role, to, h, d, only=None):
        z_copies[to, h] = send(
            z_out.at[role - 1, rows[h]], z_in.at[to, rows[h]],
            z_s.at[to, h], z_r.at[to, h], "tp", d, only)

    def after_x(role):
        i = groups.index((role, 0))
        for h in halves:
            value = acc[i, rows[h]]
            for dx in range(1, X):
                x_copies[role, dx, h].wait_recv()
                value = value + x_in[role * (X - 1) + dx - 1, rows[h]].astype(F32)
            if role == 0 or line:
                acc[i, rows[h]] = value
            if role:
                if line:

                    def store(value=value, h=h):
                        z_out[role - 1, rows[h]] = value.astype(BF16)

                    pl.when(outer)(store)
                    z_send(role, 3 - role, h, 1, outer)
                else:
                    z_out[role - 1, rows[h]] = value.astype(BF16)
                    z_send(role, role - 1, h, role)

    def relay(role):
        i = groups.index((role, 0))
        source = {3: 0, 2: 1, 1: 3}[role]
        to, d = {3: (3, 3), 2: (4, 3), 1: (5, 1)}[role]
        for h in halves:

            def add(h=h):
                z_copies[source, h].wait_recv()
                z_out[role - 1, rows[h]] = (
                    acc[i, rows[h]] + z_in[source, rows[h]].astype(F32)).astype(BF16)

            pl.when(inner)(add)
            z_send(role, to, h, d, inner)

    due = {}
    for role in roles[:-1]:
        i = groups.index((role, 0))
        due.setdefault(i + 3, []).append(functools.partial(after_x, role))
        if line:
            due.setdefault(i + 6, []).append(functools.partial(relay, role))
    for i, (role, dx) in enumerate(groups):
        for dc in reversed(range(C)):
            b = i * C + C - 1 - dc
            o_copy(b).wait()
            rhs = obuf.at[b % SLOTS]
            if dc:
                at = i * (C - 1) + dc - 1

                def put(columns, product):
                    core_out[at, :, columns] = product.astype(BF16)

                multiply(attn, rhs, put)
                if b == 0:
                    pl.semaphore_wait(barrier, Z + X + C - 3)
                for h in halves:
                    core_copies[i, dc, h] = send(
                        core_out.at[at, rows[h]], core_in.at[at, rows[h]],
                        core_s.at[at, h], core_r.at[at, h], "tr", dc)
            else:

                def put(columns, product):
                    acc[i, :, columns] = product

                multiply(attn, rhs, put)
            if b + SLOTS < n:
                o_copy(b + SLOTS).start()
            else:
                q_copy(q_next).start()
                q_next += 1
            if dc == C - 1 and i >= 1:
                after_core(i - 1)
        for event in due.pop(i, ()):
            event()
    while q_next < n:
        q_copy(q_next).start()
        q_next += 1
    after_core(len(groups) - 1)
    for when in sorted(due):
        for event in due[when]:
            event()
    after_x(0)

    res_copy.wait()
    last = len(groups) - 1
    if line:
        for h in halves:

            def end(h=h):
                z_copies[5, h].wait_recv()
                total[rows[h]] = acc[last, rows[h]] + z_in[5, rows[h]].astype(F32)

            def middle(h=h):
                z_copies[2, h].wait_recv()
                z_copies[4, h].wait_recv()
                total[rows[h]] = (acc[last, rows[h]] + z_in[2, rows[h]].astype(F32)
                                  + z_in[4, rows[h]].astype(F32))

            pl.when(outer)(end)
            pl.when(inner)(middle)
    else:
        for h in halves:
            value = acc[last, rows[h]]
            for role in range(1, Z):
                z_copies[role - 1, h].wait_recv()
                value = value + z_in[role - 1, rows[h]].astype(F32)
            total[rows[h]] = value

    arrive = {}

    def gather(source, to, h, axis, d, only=None, add=True):
        a, b = slot(*source), slot(*to)
        s = g_s.at[b, h] if add else f_s.at[source[0], h]
        copy = send(gath.at[a, rows[h]], gath.at[b, rows[h]], s, g_r.at[b, h], axis, d, only)
        if add:
            arrive[to, h] = copy

    def spread(at, h):
        role, dx, dc = at
        if dc:
            return
        if dx == 0:
            if line:
                if role == 0:
                    gather(at, (1, 0, 0), h, "tp", 1)
                    gather(at, (2, 0, 0), h, "tp", 3, inner)
                elif role == 1:
                    gather(at, (3, 0, 0), h, "tp", 3, inner)
                else:
                    gather(at, at, h, "tp", 1, inner, add=False)
            elif role == 0:
                for to in range(1, Z):
                    gather(at, (to, 0, 0), h, "tp", to)
            for d in range(1, X):
                gather(at, (role, d, 0), h, "tq", d)
        for d in range(1, C):
            gather(at, (role, dx, d), h, "tr", d)

    for h in halves:
        hidden = (res[rows[h]].astype(F32) + total[rows[h]]).astype(BF16)
        hid[rows[h]] = hidden
        gath[0, rows[h]] = (hidden.astype(F32) * gain).astype(BF16)
        spread((0, 0, 0), h)
    widened = hid[...].astype(F32)
    gained = widened * gain
    hidden_copy = pltpu.make_async_copy(hid, hidden_hbm, small_sem.at[2])
    hidden_copy.start()

    squares = jnp.sum(widened * widened, axis=1, keepdims=True)
    top = jnp.max(jnp.abs(gained), axis=1, keepdims=True)
    wide = jnp.concatenate(
        [jnp.broadcast_to(squares, (TOK, 128)), jnp.broadcast_to(top, (TOK, 128))], axis=0)
    stat = jnp.transpose(wide)[:8, :]
    lane = lax.broadcasted_iota(jnp.int32, stat.shape, 1)
    axes = (("tr", C), ("tq", X), ("tp", Z))
    first = {"tr": 0, "tq": C - 1, "tp": C + X - 2}
    stat_copies = {}

    def stat_send(stage, stat):
        axis, size = axes[stage]
        stat_out[stage] = stat
        for d in range(1, size):
            at = first[axis] + d - 1
            stat_copies[axis, d] = send(
                stat_out.at[stage], stat_in.at[at], st_s.at[at], st_r.at[at], axis, d)

    def stat_take(stage, stat):
        axis, size = axes[stage]
        for d in range(1, size):
            stat_copies[axis, d].wait_recv()
            other = stat_in[first[axis] + d - 1]
            stat = jnp.where(lane < TOK, stat + other, jnp.maximum(stat, other))
        return stat

    stat_send(0, stat)

    k = 0
    for what, at in plan:
        if what == "take":
            for h in halves:
                arrive[at, h].wait_recv()
                spread(at, h)
            continue
        q_copy(k).wait()
        if k == 0:

            def put(columns, product):
                total[:, columns] = product
        else:

            def put(columns, product):
                total[:, columns] += product

        multiply(gath.at[slot(*at)], qbuf.at[slot(*at)], put)
        if k in (1, 3):
            stage = 0 if k == 1 else 1
            stat = stat_take(stage, stat_out[stage])
            stat_send(stage + 1, stat)
        k += 1
    stat = stat_take(2, stat_out[2])
    scale = lax.rsqrt(stat / D + 1e-05)
    peak_ref[...] = pltpu.roll(stat, TOK, 1) * scale
    column = jnp.transpose(jnp.broadcast_to(scale[:1, :], (128, 128)))[:TOK, :1]
    query_ref[...] = (total[...] * column).astype(BF16)
    hidden_copy.wait()
    for copy, only in sent:
        if only is None:
            copy.wait_send()
        else:
            pl.when(only)(copy.wait_send)


def place(hidden_in, peak_in, query_in, hidden_ref, peak_ref, query_ref):
    hidden_ref[...] = hidden_in[...]
    peak_ref[...] = peak_in[0, : peak_ref.shape[0]]
    query_ref[...] = query_in[...]


def body(sizes, attn_heads, residual, o_weight, norm_gain, q_weight):
    Z, X, C = sizes
    TOK, F = residual.shape
    K, D = o_weight.shape
    n = Z * X * C
    pairs = Z * X * (C - 1)
    dma = pltpu.SemaphoreType.DMA
    block = (TOK, F)
    hbm = pl.BlockSpec(memory_space=pl.ANY)
    vmem = pl.BlockSpec(memory_space=pltpu.VMEM)
    hops = C + X + Z - 3
    steps = 6 if Z == 4 else Z - 1
    hidden, peak, query = pl.pallas_call(
        functools.partial(kernel, Z, X, C, D),
        name="decode",
        out_shape=(
            jax.ShapeDtypeStruct(block, BF16),
            jax.ShapeDtypeStruct((8, 128), F32),
            jax.ShapeDtypeStruct(block, BF16),
        ),
        in_specs=[hbm, hbm, hbm, vmem, hbm],
        out_specs=(hbm, vmem, vmem),
        scratch_shapes=[
            pltpu.VMEM((TOK, K), BF16),
            pltpu.VMEM(block, BF16),
            pltpu.VMEM(block, BF16),
            pltpu.VMEM((SLOTS, K, F), BF16),
            pltpu.VMEM((n, F, q_weight.shape[1]), BF16),
            pltpu.VMEM((n,) + block, BF16),
            pltpu.VMEM((Z * X,) + block, F32),
            pltpu.VMEM(block, F32),
            pltpu.VMEM((pairs,) + block, BF16),
            pltpu.VMEM((pairs,) + block, BF16),
            pltpu.VMEM((Z * (X - 1),) + block, BF16),
            pltpu.VMEM((Z * (X - 1),) + block, BF16),
            pltpu.VMEM((Z - 1,) + block, BF16),
            pltpu.VMEM((steps,) + block, BF16),
            pltpu.VMEM((3, 8, 128), F32),
            pltpu.VMEM((hops, 8, 128), F32),
            dma((3,)), dma((SLOTS,)), dma((n,)),
            dma((pairs, PARTS)), dma((pairs, PARTS)),
            dma((Z * (X - 1), PARTS)), dma((Z * (X - 1), PARTS)),
            dma((steps, PARTS)), dma((steps, PARTS)),
            dma((n, PARTS)), dma((n, PARTS)), dma((4, PARTS)),
            dma((hops,)), dma((hops,)),
        ],
        compiler_params=pltpu.CompilerParams(
            collective_id=0, has_side_effects=True, vmem_limit_bytes=66 * 1000 * 1000),
    )(attn_heads, residual, o_weight, norm_gain, q_weight)
    return pl.pallas_call(
        place,
        name="place",
        out_shape=(
            jax.ShapeDtypeStruct(block, BF16),
            jax.ShapeDtypeStruct((TOK,), F32),
            jax.ShapeDtypeStruct(block, BF16),
        ),
        in_specs=[vmem] * 3,
        out_specs=(vmem,) * 3,
    )(hidden, peak, query)


def solution(mesh):
    split = ("tp", "tq", "tr")
    placed = (
        P("groups", split),
        P("groups", split),
        P(split, None),
        P(split),
        P(None, split),
    )
    return jax.shard_map(
        functools.partial(body, tuple(mesh.shape[axis] for axis in split)),
        mesh=mesh,
        in_specs=placed,
        out_specs=(P("groups", split), P("groups"), P("groups", split)),
        check_vma=False,
    )
```

time: 57.6 us -> 53.1 us (0.922)
  local copies, waits for them, and re-layouts: 5.61 us -> 0 us
  Pallas kernels: 51.1 us -> 52.3 us
    unnamed x2 -> x0, local copies, waits for them, and re-layouts: 3.13 us -> none
    pallas_call x0 -> x1, Pallas kernels: none -> 1.68 us  [body(): pl.pallas_call(place, name='place', out_shape=(jax.ShapeDtypeStruct(block...]
    reshape x1 -> x0, local copies, waits for them, and re-layouts: 1.28 us -> none  [body(): norm_gain.reshape(1, F)]
    squeeze x1 -> x0, local copies, waits for them, and re-layouts: 1.2 us -> none  [body(): return (hidden, peak[0, :TOK], query)]
where the time goes in v2:
time: 53.1 us; the launch traced here: 52.9 us
  Pallas kernels  52.3 us (98%)
  between operations  0.64 us (1%)
    pallas_call x1, Pallas kernels, body(): pl.pallas_call(functools.partial(kernel, Z, X, C, D), name='decode', out_...  50.6 us
    pallas_call x1, Pallas kernels, body(): pl.pallas_call(place, name='place', out_shape=(jax.ShapeDtypeStruct(block...  1.68 us

profile of v2, /device:TPU:0, one launch (start us, length us, event | category | flops | bytes accessed | tf_op | source)
XLA Modules:
  0.0 52.9 jit_solution(16007629024099162148)
XLA Ops:
  0.6 50.6 %decode.1 = (bf16[64,1024]{1,0:T(8,128)(2,1)}, f32[8,128]{1,0:T(8,128)}, bf16[64,1024]{1,0:T(8,128)(2,1)}) custom-call(bf16[64,1024]{1,0:T(8,128)(2,1)} %attn_hbm.1, bf16[64,1024]{1,0:T(8,128)(2,1)} %res_hbm.1, bf16[1024,16384]{1,0:T(8,128)(2,1)} %o_hbm.1, bf16[1024]{0:T(1024)(128)(2,1)} %gain_ref.1, bf16[16384,1024]{1,0:T(8,128)(2,1)} %q_hbm.1), custom_call_target="tpu_custom_call" | custom-call | tf_op jit(solution)/shard_map/decode/pallas_call | solution.py:397
  51.2 1.7 %place.1 = (bf16[64,1024]{1,0:T(8,128)(2,1)}, f32[64]{0:T(128)}, bf16[64,1024]{1,0:T(8,128)(2,1)}) custom-call(bf16[64,1024]{1,0:T(8,128)(2,1)} %get-tuple-element.6.hidden_in, f32[8,128]{1,0:T(8,128)} %get-tuple-element.7.peak_in, bf16[64,1024]{1,0:T(8,128)(2,1)} %get-tuple-element.8.query_in), custom_call_target="tpu_custom_call" | custom-call | tf_op jit(solution)/shard_map/place/pallas_call | solution.py:434
